TPU v7x, 32 devices: a whole 2x2x4 slice. The times are simulated.
32 devices in a mesh: cuts: 4 (over z), row: 8 (over y, x, core).
Axes of the slice: x: 2, y: 2, z: 4, core: 2. Of those that a mesh axis runs over, the one named last changes fastest.
Arguments:
- eigvecs: float32 [16384, 2048], P('row', 'cuts'), may hold values from -1.2 to 1.2
- slice_counts: int32 [4], P('cuts'), may hold values from 256 to 512, as said below
- occ_index: int32 [2048], P('cuts'), may hold values from 0 to 63
- occ_levels: float32 [64], replicated, may hold values from 0 to 1
Outputs:
- slab: float32 [4096, 16384], P('cuts', 'row')
Inputs may be any that keep to these rules, and one draw needn't show every extreme that they name: `slice_counts`: some slice holds exactly 512 eigenvalues in every draw; the others at least half of that.
All inputs are finite; a program needn't handle non-finite values.
Results may differ from a plain program's by a relative error of at most 0.000062.
Values sent between devices are 32-bit elements; how exact they have to be, the bound alone decides.
No kernel may reach another device: no remote copies, remote signals or barrier semaphores. Data moves between devices by JAX's collectives and lax.ppermute only.
A program may use at most 128 MiB of HBM per device.

v0:
```python
import jax
import jax.numpy as jnp
from jax import lax
from jax.sharding import PartitionSpec as P

BLOCK = 1024
SLAB_SUB = 256
SLAB = 4096


def shards(eigvecs, slice_counts, occ_index, occ_levels):
    row_count = eigvecs.shape[0]
    slot_count = eigvecs.shape[1]
    level_ids = jnp.arange(occ_levels.shape[0], dtype=jnp.int32)
    one_hot = (occ_index[:, None] == level_ids[None, :]).astype(jnp.float32)
    values = jnp.dot(one_hot, occ_levels, precision=lax.Precision.HIGHEST)
    live = jnp.arange(slot_count, dtype=jnp.int32) < slice_counts[0]
    weights = jnp.where(live, values, jnp.float32(0.0))
    local_blocks = eigvecs.reshape(row_count // BLOCK, BLOCK, slot_count)[:, :SLAB_SUB, :]
    local_rows = local_blocks.reshape(-1, slot_count) * weights[None, :]
    cut_count = lax.axis_size("cuts")
    row_devices = lax.axis_size("row")
    owned = SLAB // cut_count
    strip = slot_count // row_devices
    spread = lax.all_to_all(local_rows.T, "row", split_axis=0, concat_axis=1, tiled=True)
    owners = lax.all_to_all(spread, "cuts", split_axis=1, concat_axis=0, tiled=True)
    panels = lax.all_gather(owners, "row", axis=0, tiled=True)
    panel = (
        panels.reshape(row_devices, cut_count, strip, owned)
        .transpose(1, 0, 2, 3)
        .reshape(cut_count * slot_count, owned)
    )
    return lax.dot_general(
        panel,
        lax.all_gather(eigvecs, "cuts", axis=1, tiled=True),
        (((0,), (1,)), ((), ())),
        precision=lax.Precision.HIGHEST,
        preferred_element_type=jnp.float32,
    )


def solution(mesh):
    return jax.shard_map(
        shards,
        mesh=mesh,
        in_specs=(P("row", "cuts"), P("cuts"), P("cuts"), P()),
        out_specs=P("cuts", "row"),
        check_vma=False,
    )
```

profile of v0, /device:TPU:0, one launch (start us, length us, event | category | flops | bytes accessed | tf_op | source)
XLA Modules:
  0.0 519.5 jit_solution(15764011367793498607)
XLA Ops:
  6.5 0.0 copy-start
  6.5 0.0 all-gather.3.cloned.1.call-start
  7.2 1.3 slice.4
  8.5 0.3 copy.14
  8.8 0.0 copy-done
  8.9 1.0 fusion
  9.9 0.2 broadcast_multiply_fusion
  10.0 20.3 %all_to_all.35 = f32[8,64,512]{2,1,0:T(8,128)S(1)} all-to-all(f32[8,64,512]{2,1,0:T(8,128)S(1)} %bitcast.24), channel_id=1, replica_groups=mesh['cuts'=4,'row'=8] {'row'}, dimensions={0} | all-to-all | bytes 2097152 | tf_op jit(solution)/shard_map/all_to_all | solution.py:25
  30.3 0.6 copy.10
  31.0 0.5 all_to_all.29
  31.5 0.6 copy.11
  32.1 29.9 %all_to_all.36 = f32[64,4,1024]{2,0,1:T(8,128)} all-to-all(f32[64,4,1024]{2,0,1:T(8,128)S(1)} %copy.11), channel_id=1, replica_groups=mesh['cuts'=4,'row'=8] {'cuts'}, dimensions={1} | all-to-all | bytes 2097152 | tf_op jit(solution)/shard_map/all_to_all | solution.py:26
  62.0 0.0 all-gather.3.cloned.1.call-update
  62.1 0.0 all-gather.5.cloned.1.call-start
  62.1 0.7 all-gather.5.cloned.1.call-update
  62.8 51.5 %all-gather.3.cloned.1.call-done = f32[2048,1024]{1,0:T(8,128)} async-done(((f32[256,1024]{1,0:T(8,128)}), f32[2048,1024]{1,0:T(8,128)}) %all-gather.3.cloned.1.call-update) | async-done | bytes 8388624 | tf_op jit(solution)/shard_map/all_gather | solution.py:27
  114.3 8.3 %copy.12 = f32[8,4,64,1024]{3,2,0,1:T(8,128)} copy(f32[8,4,64,1024]{3,2,1,0:T(8,128)} %bitcast.21) | data formatting | bytes 16777216 | tf_op jit(solution)/shard_map/reshape | solution.py:29
  122.6 280.1 %all-gather.5.cloned.1.call-done = f32[2048,2048]{1,0:T(8,128)} async-done(((f32[2048,512]{1,0:T(8,128)}), f32[2048,2048]{1,0:T(8,128)}) %all-gather.5.cloned.1.call-update) | async-done | bytes 16777232 | tf_op jit(solution)/shard_map/all_gather | solution.py:35
  402.7 110.0 %fusion.4 = f32[1024,2048]{1,0:T(8,128)} fusion(f32[2048,1024]{1,0:T(8,128)} %bitcast.22, f32[2048,2048]{1,0:T(8,128)} %all-gather.5.cloned.1.call-done), kind=kOutput, calls=%fused_computation.7 | convolution fusion | flops 51539607552 | bytes 33554432 | tf_op jit(solution)/shard_map/dot_general | solution.py:33
  (1 shorter events, 0.0 us)
Async XLA Ops:
  6.5 2.3 copy-start
  6.5 107.8 %all-gather.3.cloned.1.call-start = ((), (), s32[]{:S(2)}) async-start(), calls=%async_computation.2 | async-start | bytes 9437184 | tf_op jit(solution)/shard_map/all_gather | solution.py:27
  62.1 340.6 %all-gather.5.cloned.1.call-start = ((), (), s32[]{:S(2)}) async-start(), calls=%async_computation.3 | async-start | bytes 20971520 | tf_op jit(solution)/shard_map/all_gather | solution.py:35
Sparse Core Ops, SparseCore 0:
  62.2 52.0 all-gather.2
  115.9 286.7 all-gather.4
where the time goes:
time: 520 us; the launch traced here: 519 us
  waiting for transfers between devices  332 us (64%)
  matrix products  111 us (21%)
  blocking collectives  50.3 us (10%)
  between operations  14.1 us (3%)
  local copies, waits for them, and re-layouts  11.6 us (2%)
    all_gather x1, waiting for transfers between devices, shards(): lax.all_gather(eigvecs, 'cuts', axis=1, tiled=True)  280 us
    dot_general x1, matrix products, shards(): lax.dot_general(panel, lax.all_gather(eigvecs, 'cuts', axis=1, tiled=True...  110 us
    all_gather x1, waiting for transfers between devices, shards(): panels = lax.all_gather(owners, 'row', axis=0, tiled=True)  51.5 us
    all_to_all x1, blocking collectives, shards(): lax.all_to_all(spread, 'cuts', split_axis=1, concat_axis=0, tiled=True)  29.9 us
    all_to_all x1, blocking collectives, shards(): lax.all_to_all(local_rows.T, 'row', split_axis=0, concat_axis=1, tiled=True)  20.3 us
  transfers between devices with their start and end apart: 2, of which 2 were waited for; matrix products, arithmetic and copies ran while one was open for 2% of the time, Pallas kernels for 0%

commit v1 on v0

--- a/solution.py
+++ b/solution.py
@@ -32,7 +32,7 @@
     )
     return lax.dot_general(
         panel,
-        lax.all_gather(eigvecs, "cuts", axis=1, tiled=True),
+        jnp.concatenate(lax.all_gather(eigvecs, "cuts"), axis=1),
         (((0,), (1,)), ((), ())),
         precision=lax.Precision.HIGHEST,
         preferred_element_type=jnp.float32,

time: 520 us -> 485 us (0.933)
  matrix products: 111 us -> 59.7 us
  local copies, waits for them, and re-layouts: 11.6 us -> 28 us
    dot_general x1, matrix products: 110 us -> 58.7 us  [shards(): lax.dot_general(panel, jnp.concatenate(lax.all_gather(eigvecs, 'cuts'), a...]
    reshape x0 -> x1, local copies, waits for them, and re-layouts: none -> 16.3 us  [shards(): jnp.concatenate(lax.all_gather(eigvecs, 'cuts'), axis=1)]
where the time goes in v1:
time: 485 us
  waiting for transfers between devices  332 us (68%)
  matrix products  59.7 us (12%)
  blocking collectives  50.3 us (10%)
  local copies, waits for them, and re-layouts  28 us (6%)
  between operations  14.1 us (3%)
    all_gather x1, waiting for transfers between devices, shards(): lax.all_gather(eigvecs, 'cuts')  280 us
    dot_general x1, matrix products, shards(): lax.dot_general(panel, jnp.concatenate(lax.all_gather(eigvecs, 'cuts'), a...  58.7 us
    all_gather x1, waiting for transfers between devices, shards(): panels = lax.all_gather(owners, 'row', axis=0, tiled=True)  51.5 us
    all_to_all x1, blocking collectives, shards(): lax.all_to_all(spread, 'cuts', split_axis=1, concat_axis=0, tiled=True)  29.9 us
    all_to_all x1, blocking collectives, shards(): lax.all_to_all(local_rows.T, 'row', split_axis=0, concat_axis=1, tiled=True)  20.3 us
    reshape x1, local copies, waits for them, and re-layouts, shards(): jnp.concatenate(lax.all_gather(eigvecs, 'cuts'), axis=1)  16.3 us
  transfers between devices with their start and end apart: 2, of which 2 were waited for; matrix products, arithmetic and copies ran while one was open for 2% of the time, Pallas kernels for 0%

profile of v1, /device:TPU:0, one launch (start us, length us, event | category | flops | bytes accessed | tf_op | source)
XLA Modules:
  0.0 484.6 jit_solution(17889771841809579539)
XLA Ops:
  6.5 0.0 copy-start
  6.5 0.0 all-gather.4.cloned.1.call-start
  6.5 1.3 slice.4
  7.8 0.3 copy.20
  8.8 0.0 copy-done
  8.8 1.0 fusion
  9.8 0.2 broadcast_multiply_fusion
  10.0 20.3 %all_to_all.35 = f32[8,64,512]{2,1,0:T(8,128)S(1)} all-to-all(f32[8,64,512]{2,1,0:T(8,128)S(1)} %bitcast.30), channel_id=1, replica_groups=mesh['cuts'=4,'row'=8] {'row'}, dimensions={0} | all-to-all | bytes 2097152 | tf_op jit(solution)/shard_map/all_to_all | solution.py:25
  30.3 0.6 copy.15
  30.9 0.5 all_to_all.29
  31.5 0.6 copy.16
  32.1 29.9 %all_to_all.36 = f32[64,4,1024]{2,0,1:T(8,128)} all-to-all(f32[64,4,1024]{2,0,1:T(8,128)S(1)} %copy.16), channel_id=1, replica_groups=mesh['cuts'=4,'row'=8] {'cuts'}, dimensions={1} | all-to-all | bytes 2097152 | tf_op jit(solution)/shard_map/all_to_all | solution.py:26
  62.0 0.0 all-gather.4.cloned.1.call-update
  62.1 0.0 all-gather.6.cloned.1.call-start
  62.1 0.7 all-gather.6.cloned.1.call-update
  62.8 51.5 %all-gather.4.cloned.1.call-done = f32[2048,1024]{1,0:T(8,128)} async-done(((f32[256,1024]{1,0:T(8,128)}), f32[2048,1024]{1,0:T(8,128)}) %all-gather.4.cloned.1.call-update) | async-done | bytes 8388624 | tf_op jit(solution)/shard_map/all_gather | solution.py:27
  114.3 8.3 %copy.17 = f32[8,4,64,1024]{3,2,0,1:T(8,128)} copy(f32[8,4,64,1024]{3,2,1,0:T(8,128)} %bitcast.27) | data formatting | bytes 16777216 | tf_op jit(solution)/shard_map/reshape | solution.py:29
  122.6 280.1 %all-gather.6.cloned.1.call-done = f32[8192,512]{1,0:T(8,128)} async-done(((f32[2048,512]{1,0:T(8,128)}), f32[8192,512]{1,0:T(8,128)}) %all-gather.6.cloned.1.call-update) | async-done | bytes 16777232 | tf_op jit(solution)/shard_map/all_gather | solution.py:35
  402.7 16.3 %copy.18 = f32[2048,4,512]{0,2,1:T(8,128)} copy(f32[2048,4,512]{2,0,1:T(8,128)} %bitcast.25) | data formatting | bytes 33554432 | tf_op jit(solution)/shard_map/reshape | solution.py:35
  419.0 0.0 copy-start.1
  419.0 58.7 %fusion.4 = f32[1024,2048]{1,0:T(8,128)} fusion(f32[2048,1024]{1,0:T(8,128)} %bitcast.28, f32[2048,2048]{0,1:T(8,128)} %bitcast.26), kind=kOutput, calls=%fused_computation.7 | convolution fusion | flops 51539607552 | bytes 33554432 | tf_op jit(solution)/shard_map/dot_general | solution.py:33
  477.7 0.0 copy-done.1
  (1 shorter events, 0.0 us)
Async XLA Ops:
  6.5 2.3 copy-start
  6.5 107.8 %all-gather.4.cloned.1.call-start = ((), (), s32[]{:S(2)}) async-start(), calls=%async_computation.2 | async-start | bytes 9437184 | tf_op jit(solution)/shard_map/all_gather | solution.py:27
  62.1 340.6 %all-gather.6.cloned.1.call-start = ((), (), s32[]{:S(2)}) async-start(), calls=%async_computation.3 | async-start | bytes 20971520 | tf_op jit(solution)/shard_map/all_gather | solution.py:35
  419.0 58.7 %copy-start.1 = (f32[64]{0:T(128)S(1)}, f32[64]{0:T(128)}, u32[]{:S(2)}) copy-start(f32[64]{0:T(128)} %param.7) | copy-start | bytes 772
Sparse Core Ops, SparseCore 0:
  62.2 52.0 all-gather.3
  115.9 286.7 all-gather.5
